TPU v7x, 512 devices: a whole 4x8x8 slice. The times are simulated.
512 devices in a mesh: row: 8 (over y), col: 16 (over z, core), rhs: 4 (over x).
Axes of the slice: x: 4, y: 8, z: 8, core: 2. Of those that a mesh axis runs over, the one named last changes fastest.
Arguments:
- points: bfloat16 [64, 786432], P(None, ('row', 'col')), may hold values from -6 to 6
- vectors: bfloat16 [64, 786432], P('rhs', ('row', 'col')), may hold values from -6 to 6
- leaf_basis: bfloat16 [1536, 512, 128], P(('row', 'col')), may hold values from -0.25 to 0.25
- leaf_transfer: bfloat16 [1536, 128, 128], P(('row', 'col')), may hold values from -0.375 to 0.375
- node_transfer: bfloat16 [128, 128, 128], P(('row', 'col')), may hold values from -0.375 to 0.375
- leaf_coupling: bfloat16 [1536, 3, 128, 128], P(('row', 'col')), may hold values from -0.3125 to 0.3125
- node_coupling: bfloat16 [128, 6, 128, 128], P(('row', 'col')), may hold values from -0.09375 to 0.09375
- top_coupling: bfloat16 [16, 16, 128, 128], P('col'), may hold values from -0.02734375 to 0.02734375
- near_list: int32 [1536, 5], P(('row', 'col')), may hold values from 0 to 1535, as said below
- near_count: int32 [1536], P(('row', 'col')), may hold values from 1 to 5, as said below
- far_leaves: int32 [1536, 3], P(('row', 'col')), may hold values from 0 to 1535, as said below
- far_nodes: int32 [128, 6], P(('row', 'col')), may hold values from 0 to 127, as said below
Outputs:
- product: bfloat16 [64, 786432], P('rhs', ('row', 'col'))
Inputs may be any that keep to these rules, and one draw needn't show every extreme that they name: `near_list`: the first entry of row l is l itself; all entries of a row are distinct and lie in the window of leaves j with (j // 12 - l // 12) mod (128) in the finite set (-1, 0, 1), cyclically. Entries from near_count[l] on are not used. `near_count`: some leaf has 5 used entries. `far_leaves`: entries of a row are distinct, lie in the same cyclic window as the near rows, and differ from all 5 entries of the leaf's near row. `far_nodes`: entries of a row are distinct and never the node itself.
All inputs are finite; a program needn't handle non-finite values.
Results may differ from a plain program's by a relative error of at most 0.01.
Values may be sent and summed in bfloat16 or wider, within the bound.
A program may use at most 64 MiB of HBM per device.

v0:
```python
import jax
import jax.numpy as jnp
from jax import lax
from jax.sharding import PartitionSpec as P

pair_group = 8


def with_halo(array, sides, width):
    edges = {}
    for axis, dim in sides:
        peers, length = (lax.axis_size(axis), array.shape[dim])
        up = [(i, (i + 1) % peers) for i in range(peers)]
        last = lax.slice_in_dim(array, length - width, length, axis=dim)
        initial = lax.slice_in_dim(array, 0, width, axis=dim)
        edges[dim] = (
            lax.ppermute(last, axis, up),
            lax.ppermute(initial, axis, [(b, a) for a, b in up]),
        )
    done = []
    for _, dim in sides:
        low, high = edges[dim]
        around = [(width, width) if d in done else (0, 0) for d in range(array.ndim)]
        array = jnp.concatenate([jnp.pad(low, around), array, jnp.pad(high, around)], axis=dim)
        done.append(dim)
    return array


def in_order(pieces, dim):
    pieces = jnp.moveaxis(pieces, 0, dim)
    dims = pieces.shape
    return pieces.reshape(*dims[:dim], dims[dim] * dims[dim + 1], *dims[dim + 2 :])


def gather_packed(arrays, axis, dims):
    line = jnp.concatenate([a.reshape(-1) for a in arrays])
    lines, at, gathered = (lax.all_gather(line, axis), 0, [])
    for a, dim in zip(arrays, dims):
        pieces = lines[:, at : at + a.size].reshape(-1, *a.shape)
        gathered.append(in_order(pieces, dim))
        at += a.size
    return tuple(gathered)


def near_field(
    extended, features, near_count, near_list, window_start, leaf_total, first_pair, stride
):
    leaves_here = near_count.shape[0]
    slot_count = near_list.shape[1]
    leaf_len = extended.shape[1] // (3 * leaves_here)
    stacked_all = extended.reshape(extended.shape[0], 3 * leaves_here, leaf_len)
    columns = extended.shape[0] - features
    center_points = stacked_all[:features, leaves_here : 2 * leaves_here]
    is_valid = (jnp.arange(slot_count)[None, :] < near_count[:, None]).reshape(-1)
    ordering = jnp.argsort(jnp.where(is_valid, 0, 1).astype(jnp.int32), stable=True)
    live_total = jnp.sum(is_valid.astype(jnp.int32))
    targets = ordering // slot_count
    sources = (near_list.reshape(-1)[ordering] - window_start) % leaf_total
    my_pairs = jnp.maximum(live_total - first_pair + stride - 1, 0) // stride
    turn_count = (my_pairs + pair_group - 1) // pair_group
    window_ids = jnp.arange(3 * leaves_here, dtype=jnp.int32)
    own_ids = jnp.arange(leaves_here, dtype=jnp.int32)

    def one_turn(turn_idx, accum_near):
        pair_rank = turn_idx * pair_group + jnp.arange(pair_group, dtype=jnp.int32)
        is_live = (pair_rank < my_pairs).astype(jnp.float32)
        picks = jnp.minimum(first_pair + stride * pair_rank, leaves_here * slot_count - 1)
        targets_now = targets[picks]
        sources_now = sources[picks]
        pick_source = (sources_now[:, None] == window_ids[None, :]).astype(jnp.bfloat16)
        pick_target = (targets_now[:, None] == own_ids[None, :]).astype(jnp.bfloat16)
        chosen = jnp.einsum(
            "gn,knb->kgb", pick_source, stacked_all, preferred_element_type=jnp.float32
        ).astype(jnp.bfloat16)
        source_points = chosen[:features]
        source_values = chosen[features:]
        target_points = jnp.einsum(
            "gn,fnb->fgb", pick_target, center_points, preferred_element_type=jnp.float32
        ).astype(jnp.bfloat16)
        source_wide = source_points.astype(jnp.float32)
        target_wide = target_points.astype(jnp.float32)
        source_squares = jnp.sum(source_wide * source_wide, axis=0)
        target_squares = jnp.sum(target_wide * target_wide, axis=0)
        crossed = jnp.einsum(
            "fgb,fga->gba", source_points, target_points, preferred_element_type=jnp.float32
        )
        distance = source_squares[:, :, None] + target_squares[:, None, :] - 2.0 * crossed
        kernel_tile = jnp.exp(distance * (-2.0 / features)).astype(jnp.bfloat16)
        contrib = jnp.einsum(
            "cgb,gba->cga", source_values, kernel_tile, preferred_element_type=jnp.float32
        )
        placing = pick_target.astype(jnp.float32) * is_live[:, None]
        return accum_near + jnp.einsum("cga,gn->cna", contrib, placing)

    accum_near = lax.fori_loop(
        0, turn_count, one_turn, jnp.zeros((columns, leaves_here, leaf_len), jnp.float32)
    )
    return accum_near.reshape(columns, leaves_here * leaf_len)


def local(
    points,
    vectors,
    leaf_basis,
    leaf_transfer,
    node_transfer,
    leaf_coupling,
    node_coupling,
    top_coupling,
    near_list,
    near_count,
    far_leaves,
    far_nodes,
):
    device_count = lax.axis_size(("row", "col"))
    device = lax.axis_index(("row", "col"))
    leaves_here = near_count.shape[0]
    leaf_total = leaves_here * device_count
    window_start = (device - 1) * leaves_here
    leaf_len = leaf_basis.shape[1]
    rank_dim = leaf_basis.shape[2]
    columns = vectors.shape[0]
    features = points.shape[0]
    first_pair = 0
    stride = 1
    stacked = jnp.concatenate([points, vectors], axis=0)
    extended = with_halo(stacked, ((("row", "col"), 1),), leaves_here * leaf_len)
    blocks = vectors.reshape(columns, leaves_here, leaf_len)
    moments = jnp.einsum(
        "cnl,nlk->cnk", blocks, leaf_basis, preferred_element_type=jnp.float32
    ).astype(jnp.bfloat16)
    moment_cycle = with_halo(
        moments.reshape(columns, leaves_here * rank_dim),
        ((("row", "col"), 1),),
        leaves_here * rank_dim,
    )
    moment_cycle = moment_cycle.reshape(columns, 3 * leaves_here, rank_dim)
    node_moments = jnp.einsum(
        "cnr,nrs->cs", moments, leaf_transfer, preferred_element_type=jnp.float32
    ).astype(jnp.bfloat16)
    lifted = jnp.dot(node_moments, node_transfer[0], preferred_element_type=jnp.float32).astype(
        jnp.bfloat16
    )
    everyone, lifted_all = gather_packed((node_moments[None], lifted[None]), ("row", "col"), (0, 0))
    col_count = lax.axis_size("col")
    top_moments = jnp.sum(
        lifted_all.astype(jnp.float32).reshape(-1, col_count, columns, rank_dim), axis=0
    ).astype(jnp.bfloat16)
    near_part = near_field(
        extended, features, near_count, near_list, window_start, leaf_total, first_pair, stride
    )
    far_pos = (far_leaves - window_start) % leaf_total
    picked = moment_cycle[:, far_pos]
    leaf_field = jnp.einsum(
        "cnkr,nkrs->cns", picked, leaf_coupling, preferred_element_type=jnp.float32
    )
    node_field = jnp.einsum(
        "kcr,krs->cs", everyone[far_nodes[0]], node_coupling[0], preferred_element_type=jnp.float32
    )
    top_field = jnp.einsum(
        "jcr,jrs->cs", top_moments, top_coupling[0], preferred_element_type=jnp.float32
    ).astype(jnp.bfloat16)
    lowered_top = lax.dot_general(
        top_field, node_transfer[0], (((1,), (1,)), ((), ())), preferred_element_type=jnp.float32
    )
    node_down = (node_field + lowered_top).astype(jnp.bfloat16)
    lowered_node = jnp.einsum(
        "cs,nrs->cnr", node_down, leaf_transfer, preferred_element_type=jnp.float32
    )
    leaf_down = (leaf_field + lowered_node).astype(jnp.bfloat16)
    far_part = jnp.einsum(
        "cnr,nlr->cnl", leaf_down, leaf_basis, preferred_element_type=jnp.float32
    ).reshape(columns, leaves_here * leaf_len)
    return (near_part + far_part).astype(jnp.bfloat16)


def solution(mesh):
    return jax.shard_map(
        local,
        mesh=mesh,
        in_specs=(
            P(None, ("row", "col")),
            P("rhs", ("row", "col")),
            P(("row", "col"), None, None),
            P(("row", "col"), None, None),
            P(("row", "col"), None, None),
            P(("row", "col"), None, None, None),
            P(("row", "col"), None, None, None),
            P("col", None, None, None),
            P(("row", "col"), None),
            P(("row", "col")),
            P(("row", "col"), None),
            P(("row", "col"), None),
        ),
        out_specs=P("rhs", ("row", "col")),
        check_vma=False,
    )
```

profile of v0, /device:TPU:1, one launch (start us, length us, event | category | flops | bytes accessed | tf_op | source)
XLA Modules:
  0.0 122.9 jit_solution(6125616809375461619)
XLA Ops:
  6.6 1.3 %constant_dynamic-update-slice_fusion.1 = bf16[80,6144]{1,0:T(8,128)(2,1)S(1)} fusion(bf16[64,6144]{1,0:T(8,128)(2,1)} %param.14), kind=kLoop, calls=%fused_computation.82 | loop fusion | bytes 1572864
  7.9 0.9 constant_dynamic-update-slice_fusion
  8.9 5.4 %collective-permute-start = (bf16[80,6144]{1,0:T(8,128)(2,1)S(1)}, bf16[80,6144]{1,0:T(8,128)(2,1)}, u32[]{:S(2)}, u32[]{:S(2)}) collective-permute-start(bf16[80,6144]{1,0:T(8,128)(2,1)S(1)} %constant_dynamic-update-slice_fusion), channel_id=1, source_target_pairs={{0,4},{4,8},{8,12},{12,16},{16,20},{20,24},{24,28},{28,32},{32,36}... | collective-permute-start | bytes 2949128 | tf_op jit(solution)/shard_map/ppermute | solution.py:17
  14.3 5.3 %collective-permute-start.1 = (bf16[80,6144]{1,0:T(8,128)(2,1)S(1)}, bf16[80,6144]{1,0:T(8,128)(2,1)}, u32[]{:S(2)}, u32[]{:S(2)}) collective-permute-start(bf16[80,6144]{1,0:T(8,128)(2,1)S(1)} %constant_dynamic-update-slice_fusion), channel_id=1, source_target_pairs={{4,0},{8,4},{12,8},{16,12},{20,16},{24,20},{28,24},{32,28},{36,32}... | collective-permute-start | bytes 2949128 | tf_op jit(solution)/shard_map/ppermute | solution.py:18
  19.6 1.2 %convolution_convert_fusion.2 = bf16[12,128,16]{1,2,0:T(8,128)(2,1)S(1)} fusion(bf16[12,512,128]{2,1,0:T(8,128)(2,1)S(1)} %copy-done, bf16[2,12,8,512]{3,2,1,0:T(8,128)(2,1)} %bitcast.144), kind=kOutput, calls=%fused_computation.49 | convolution fusion | flops 25190400 | bytes 1818624 | tf_op jit(solution)/shard_map/cnl,nlk->cnk/dot_general | solution.py:129
  20.8 7.9 %collective-permute-start.3 = (bf16[16,1536]{1,0:T(8,128)(2,1)S(1)}, bf16[16,1536]{1,0:T(8,128)(2,1)S(1)}, u32[]{:S(2)}, u32[]{:S(2)}) collective-permute-start(bf16[16,1536]{1,0:T(8,128)(2,1)S(1)} %copy_bitcast_fusion), channel_id=1, source_target_pairs={{4,0},{8,4},{12,8},{16,12},{20,16},{24,20},{28,24},{32,28},{36,32}... | collective-permute-start | bytes 147464 | tf_op jit(solution)/shard_map/ppermute | solution.py:18
  28.8 1.9 %collective-permute-start.2 = (bf16[16,1536]{1,0:T(8,128)(2,1)S(1)}, bf16[16,1536]{1,0:T(8,128)(2,1)S(1)}, u32[]{:S(2)}, u32[]{:S(2)}) collective-permute-start(bf16[16,1536]{1,0:T(8,128)(2,1)S(1)} %copy_bitcast_fusion), channel_id=1, source_target_pairs={{0,4},{4,8},{8,12},{12,16},{16,20},{20,24},{24,28},{28,32},{32,36}... | collective-permute-start | bytes 147464 | tf_op jit(solution)/shard_map/ppermute | solution.py:17
  31.0 0.6 pad_maximum_fusion.2
  31.7 0.7 fusion.50
  32.5 2.1 %sort.17 = (s32[60]{0:T(128)}, s32[60]{0:T(128)S(1)}) sort(s32[60]{0:T(128)S(1)} %select_n.59, s32[60]{0:T(128)S(1)} %iota.22), dimensions={0}, to_apply=%region_1.2 | sort | flops 360 | bytes 960 | tf_op jit(solution)/shard_map/jit(argsort)/sort | solution.py:55
  34.8 0.8 gather_fusion.2
  36.6 1.3 %gather_fusion.3 = bf16[36,16,128]{2,1,0:T(8,128)(2,1)} fusion(bf16[16,36,128]{2,0,1:T(8,128)(2,1)S(1)} %pad_maximum_fusion.1, s32[1024]{0:T(1024)S(1)} %get-tuple-element.106), kind=kCustom, calls=%fused_computation.3 | custom fusion | bytes 295056 | tf_op jit(solution)/shard_map/gather | solution.py:153
  37.9 3.3 %pad_maximum_fusion = bf16[80,18432]{1,0:T(8,128)(2,1)} fusion(bf16[80,6144]{1,0:T(8,128)(2,1)} %collective-permute-done.1, bf16[80,6144]{1,0:T(8,128)(2,1)S(1)} %constant_dynamic-update-slice_fusion, bf16[80,6144]{1,0:T(8,128)(2,1)} %collective-permute-done), kind=kLoop, calls=%fused_computation.41 | loop fusion | flops 8847360 | bytes 5898240 | tf_op jit(solution)/shard_map/concatenate | solution.py:24
  41.2 5.7 %reshape.91 = bf16[80,36,512]{2,1,0:T(8,128)(2,1)} reshape(bf16[80,18432]{1,0:T(8,128)(2,1)} %pad_maximum_fusion) | data formatting | bytes 5898240 | tf_op jit(solution)/shard_map/reshape | solution.py:51
  46.9 1.9 %slice.32 = bf16[64,12,512]{2,1,0:T(8,128)(2,1)S(1)} slice(bf16[80,36,512]{2,1,0:T(8,128)(2,1)} %reshape.91), slice={[0:64], [12:24], [0:512]} | slice | bytes 1572864 | tf_op jit(solution)/shard_map/slice | solution.py:53
  48.8 42.6 %while.11 = (s32[]{:T(128)}, f32[16,12,512]{2,1,0:T(8,128)S(1)}, s32[]{:T(128)}, s32[60]{0:T(128)S(1)}, s32[]{:T(128)}, /*index=5*/s32[60]{0:T(128)S(1)}, bf16[8...) while((s32[]{:T(128)}, f32[16,12,512]{2,1,0:T(8,128)S(1)}, ...), condition=%wide.region_5.6_spmd.clone, body=%wide.region_2.5_spmd.clone.sunk | while | flops 379742016 | bytes 9048605 | solution.py:95
  48.9 0.6 gather_fusion.1
  49.5 2.6 %fusion.90 = bf16[80,8,512]{2,1,0:T(8,128)(2,1)S(1)} fusion(bf16[80,36,512]{2,1,0:T(8,128)(2,1)} %get-tuple-element.187, s32[8]{0:T(128)S(1)} %gather_fusion.1), kind=kOutput, calls=%fused_computation.12.clone.1 | convolution fusion | flops 23920928 | bytes 3604512 | tf_op jit(solution)/shard_map/while/body/gn,knb->kgb/dot_general | solution.py:72
  52.1 0.8 slice.46
  53.1 0.6 gather_fusion
  53.7 1.2 multiply_reduce_fusion.4
  54.9 4.2 %fusion.91 = bf16[16,8,512]{2,0,1:T(8,128)(2,1)S(1)} fusion(f32[8,512]{1,0:T(8,128)S(1)} %get-tuple-element.159, f32[8,512]{1,0:T(8,128)S(1)} %multiply_reduce_fusion.5, bf16[64,8,512]{2,1,0:T(8,128)(2,1)} %get-tuple-element.160, bf16[64,8,512]{2,1,0:T(8,128)(2,1)} %slice.46, bf16[16,8,512]{2,1,0:T(8,128)(2,1)S(1)} %slice.47), kind=kOutput, calls=%fused_computation.16.clone.1 | convolution fusion | flops 346030080 | bytes 1343488 | tf_op jit(solution)/shard_map/while/body/cgb,gba->cga/dot_general | solution.py:89
  59.1 0.4 fusion.92
  59.5 0.6 gather_fusion.1
  60.2 2.6 %fusion.90 = bf16[80,8,512]{2,1,0:T(8,128)(2,1)S(1)} fusion(bf16[80,36,512]{2,1,0:T(8,128)(2,1)} %get-tuple-element.187, s32[8]{0:T(128)S(1)} %gather_fusion.1), kind=kOutput, calls=%fused_computation.12.clone.1 | convolution fusion | flops 23920928 | bytes 3604512 | tf_op jit(solution)/shard_map/while/body/gn,knb->kgb/dot_general | solution.py:72
  62.7 0.8 slice.46
  63.7 0.6 gather_fusion
  64.3 1.2 multiply_reduce_fusion.4
  65.5 4.2 %fusion.91 = bf16[16,8,512]{2,0,1:T(8,128)(2,1)S(1)} fusion(f32[8,512]{1,0:T(8,128)S(1)} %get-tuple-element.159, f32[8,512]{1,0:T(8,128)S(1)} %multiply_reduce_fusion.5, bf16[64,8,512]{2,1,0:T(8,128)(2,1)} %get-tuple-element.160, bf16[64,8,512]{2,1,0:T(8,128)(2,1)} %slice.46, bf16[16,8,512]{2,1,0:T(8,128)(2,1)S(1)} %slice.47), kind=kOutput, calls=%fused_computation.16.clone.1 | convolution fusion | flops 346030080 | bytes 1343488 | tf_op jit(solution)/shard_map/while/body/cgb,gba->cga/dot_general | solution.py:89
  70.2 0.6 gather_fusion.1
  70.8 2.6 %fusion.90 = bf16[80,8,512]{2,1,0:T(8,128)(2,1)S(1)} fusion(bf16[80,36,512]{2,1,0:T(8,128)(2,1)} %get-tuple-element.187, s32[8]{0:T(128)S(1)} %gather_fusion.1), kind=kOutput, calls=%fused_computation.12.clone.1 | convolution fusion | flops 23920928 | bytes 3604512 | tf_op jit(solution)/shard_map/while/body/gn,knb->kgb/dot_general | solution.py:72
  73.4 0.8 slice.46
  74.4 0.6 gather_fusion
  75.0 1.2 multiply_reduce_fusion.4
  76.2 4.2 %fusion.91 = bf16[16,8,512]{2,0,1:T(8,128)(2,1)S(1)} fusion(f32[8,512]{1,0:T(8,128)S(1)} %get-tuple-element.159, f32[8,512]{1,0:T(8,128)S(1)} %multiply_reduce_fusion.5, bf16[64,8,512]{2,1,0:T(8,128)(2,1)} %get-tuple-element.160, bf16[64,8,512]{2,1,0:T(8,128)(2,1)} %slice.46, bf16[16,8,512]{2,1,0:T(8,128)(2,1)S(1)} %slice.47), kind=kOutput, calls=%fused_computation.16.clone.1 | convolution fusion | flops 346030080 | bytes 1343488 | tf_op jit(solution)/shard_map/while/body/cgb,gba->cga/dot_general | solution.py:89
  80.8 0.6 gather_fusion.1
  81.4 2.6 %fusion.90 = bf16[80,8,512]{2,1,0:T(8,128)(2,1)S(1)} fusion(bf16[80,36,512]{2,1,0:T(8,128)(2,1)} %get-tuple-element.187, s32[8]{0:T(128)S(1)} %gather_fusion.1), kind=kOutput, calls=%fused_computation.12.clone.1 | convolution fusion | flops 23920928 | bytes 3604512 | tf_op jit(solution)/shard_map/while/body/gn,knb->kgb/dot_general | solution.py:72
  84.0 0.8 slice.46
  85.0 0.6 gather_fusion
  85.6 1.2 multiply_reduce_fusion.4
  86.8 4.2 %fusion.91 = bf16[16,8,512]{2,0,1:T(8,128)(2,1)S(1)} fusion(f32[8,512]{1,0:T(8,128)S(1)} %get-tuple-element.159, f32[8,512]{1,0:T(8,128)S(1)} %multiply_reduce_fusion.5, bf16[64,8,512]{2,1,0:T(8,128)(2,1)} %get-tuple-element.160, bf16[64,8,512]{2,1,0:T(8,128)(2,1)} %slice.46, bf16[16,8,512]{2,1,0:T(8,128)(2,1)S(1)} %slice.47), kind=kOutput, calls=%fused_computation.16.clone.1 | convolution fusion | flops 346030080 | bytes 1343488 | tf_op jit(solution)/shard_map/while/body/cgb,gba->cga/dot_general | solution.py:89
  91.4 16.7 %all-gather.3.cloned.1.call-done = bf16[524288]{0:T(1024)(128)(2,1)} async-done(((bf16[4096]{0:T(1024)(128)(2,1)}), bf16[524288]{0:T(1024)(128)(2,1)}) %all-gather.3.cloned.1.call-update) | async-done | bytes 1048592 | tf_op jit(solution)/shard_map/all_gather | solution.py:37
  108.1 1.5 %reshape.134 = bf16[128,4096]{1,0:T(8,128)(2,1)S(1)} reshape(bf16[524288]{0:T(1024)(128)(2,1)} %all-gather.3.cloned.1.call-done) | data formatting | bytes 2097152 | tf_op jit(solution)/shard_map/all_gather | solution.py:37
  110.1 0.6 gather_fusion.4
  110.7 1.1 convolution_bitcast_fusion.3
  111.7 1.4 %fusion.42 = bf16[16,128,1]{1,0,2:T(8,128)(2,1)S(1)} fusion(f32[16,128]{1,0:T(8,128)S(1)} %convolution_bitcast_fusion.3, bf16[16,16,128]{2,1,0:T(8,128)(2,1)S(1)} %bitcast_reduce_fusion, bf16[1,16,128,128]{3,2,1,0:T(8,128)(2,1)} %param.21, bf16[1,128,128]{2,1,0:T(8,128)(2,1)} %param.18), kind=kOutput, calls=%fused_computation.59 | convolution fusion | flops 8919040 | bytes 634880 | tf_op jit(solution)/shard_map/dot_general | solution.py:163
  113.3 2.0 %fusion.35 = bf16[12,2,8,512]{3,2,1,0:T(8,128)(2,1)S(1)} fusion(bf16[12,512,128]{2,1,0:T(8,128)(2,1)S(1)} %copy-done, f32[16,12,128]{2,0,1:T(8,128)S(1)} %fusion.53, bf16[16,12,3,128]{3,0,2,1:T(8,128)(2,1)S(1)} %bitcast.143, bf16[12,3,128,128]{3,2,1,0:T(8,128)(2,1)} %param.19, f32[16,12,512]{2,1,0:T(8,128)S(1)} %get-tuple-element.60), kind=kOutput, calls=%fused_computation.45 | convolution fusion | flops 44285952 | bytes 3588096 | tf_op jit(solution)/shard_map/cnr,nlr->cnl/dot_general | solution.py:171
  115.4 0.7 copy.54
  (71 shorter events, 3.4 us)
Async XLA Ops:
  6.5 13.0 %copy-start = (bf16[12,512,128]{2,1,0:T(8,128)(2,1)S(1)}, bf16[12,512,128]{2,1,0:T(8,128)(2,1)}, u32[]{:S(2)}) copy-start(bf16[12,512,128]{2,1,0:T(8,128)(2,1)} %param.16) | copy-start | bytes 4718596
  6.5 24.2 %copy-start.1 = (bf16[12,128,128]{2,1,0:T(8,128)(2,1)S(1)}, bf16[12,128,128]{2,1,0:T(8,128)(2,1)}, u32[]{:S(2)}) copy-start(bf16[12,128,128]{2,1,0:T(8,128)(2,1)} %param.17) | copy-start | bytes 1179652
  6.5 24.3 %copy-start.4 = (bf16[1,128,128]{2,1,0:T(8,128)(2,1)S(1)}, bf16[1,128,128]{2,1,0:T(8,128)(2,1)}, u32[]{:S(2)}) copy-start(bf16[1,128,128]{2,1,0:T(8,128)(2,1)} %param.18) | copy-start | bytes 98308
  6.5 25.1 %copy-start.7 = (s32[12]{0:T(128)S(1)}, s32[12]{0:T(128)}, u32[]{:S(2)}) copy-start(s32[12]{0:T(128)} %param.23) | copy-start | bytes 148
  6.5 28.1 %copy-start.5 = (s32[12,5]{0,1:T(8,128)S(1)}, s32[12,5]{0,1:T(8,128)}, u32[]{:S(2)}) copy-start(s32[12,5]{0,1:T(8,128)} %param.22) | copy-start | bytes 724
  6.5 29.0 %copy-start.6 = (s32[12,3]{0,1:T(4,128)S(1)}, s32[12,3]{0,1:T(4,128)}, u32[]{:S(2)}) copy-start(s32[12,3]{0,1:T(4,128)} %param.24) | copy-start | bytes 436
  6.6 29.2 %copy-start.8 = (s32[1,6]{1,0:T(1,128)S(1)}, s32[1,6]{1,0:T(1,128)}, u32[]{:S(2)}) copy-start(s32[1,6]{1,0:T(1,128)} %param.25) | copy-start | bytes 76
  6.6 101.6 %all-gather.3.cloned.1.call-start = ((), (), s32[]{:S(2)}) async-start(), calls=%async_computation | async-start | bytes 1056768 | tf_op jit(solution)/shard_map/all_gather | solution.py:37
  8.9 29.0 %collective-permute-start = (bf16[80,6144]{1,0:T(8,128)(2,1)S(1)}, bf16[80,6144]{1,0:T(8,128)(2,1)}, u32[]{:S(2)}, u32[]{:S(2)}) collective-permute-start(bf16[80,6144]{1,0:T(8,128)(2,1)S(1)} %constant_dynamic-update-slice_fusion), channel_id=1, source_target_pairs={{0,4},{4,8},{8,12},{12,16},{16,20},{20,24},{24,28},{28,32},{32,36}... | collective-permute-start | bytes 2949128 | tf_op jit(solution)/shard_map/ppermute | solution.py:17
  14.3 23.6 %collective-permute-start.1 = (bf16[80,6144]{1,0:T(8,128)(2,1)S(1)}, bf16[80,6144]{1,0:T(8,128)(2,1)}, u32[]{:S(2)}, u32[]{:S(2)}) collective-permute-start(bf16[80,6144]{1,0:T(8,128)(2,1)S(1)} %constant_dynamic-update-slice_fusion), channel_id=1, source_target_pairs={{4,0},{8,4},{12,8},{16,12},{20,16},{24,20},{28,24},{32,28},{36,32}... | collective-permute-start | bytes 2949128 | tf_op jit(solution)/shard_map/ppermute | solution.py:18
  20.8 15.7 %collective-permute-start.3 = (bf16[16,1536]{1,0:T(8,128)(2,1)S(1)}, bf16[16,1536]{1,0:T(8,128)(2,1)S(1)}, u32[]{:S(2)}, u32[]{:S(2)}) collective-permute-start(bf16[16,1536]{1,0:T(8,128)(2,1)S(1)} %copy_bitcast_fusion), channel_id=1, source_target_pairs={{4,0},{8,4},{12,8},{16,12},{20,16},{24,20},{28,24},{32,28},{36,32}... | collective-permute-start | bytes 147464 | tf_op jit(solution)/shard_map/ppermute | solution.py:18
  28.8 7.8 %collective-permute-start.2 = (bf16[16,1536]{1,0:T(8,128)(2,1)S(1)}, bf16[16,1536]{1,0:T(8,128)(2,1)S(1)}, u32[]{:S(2)}, u32[]{:S(2)}) collective-permute-start(bf16[16,1536]{1,0:T(8,128)(2,1)S(1)} %copy_bitcast_fusion), channel_id=1, source_target_pairs={{0,4},{4,8},{8,12},{12,16},{16,20},{20,24},{24,28},{28,32},{32,36}... | collective-permute-start | bytes 147464 | tf_op jit(solution)/shard_map/ppermute | solution.py:17
  109.7 3.5 %copy-start.2 = (bf16[12,128,128]{2,1,0:T(8,128)(2,1)S(1)}, bf16[12,128,128]{2,1,0:T(8,128)(2,1)}, u32[]{:S(2)}) copy-start(bf16[12,128,128]{2,1,0:T(8,128)(2,1)} %param.17) | copy-start | bytes 1179652
  109.8 3.6 %copy-start.3 = (bf16[36,16,128]{2,1,0:T(8,128)(2,1)S(1)}, bf16[36,16,128]{2,1,0:T(8,128)(2,1)}, u32[]{:S(2)}) copy-start(bf16[36,16,128]{2,1,0:T(8,128)(2,1)} %gather_fusion.3) | copy-start | bytes 442372
Sparse Core Ops, SparseCore 0:
  31.8 76.2 all-gather.2
where the time goes:
time: 124 us; the launch traced here: 123 us
  matrix products  39.4 us (32%)
  local copies, waits for them, and re-layouts  24 us (19%)
  starting transfers between devices  20.6 us (17%)
  waiting for transfers between devices  16.7 us (13%)
  between operations  14.4 us (12%)
  other arithmetic  7.53 us (6%)
    dot_general x4, matrix products, one_turn(): jnp.einsum('cgb,gba->cga', source_values, kernel_tile, preferred_element_...  16.8 us
    all_gather x1, waiting for transfers between devices, gather_packed(): lines, at, gathered = (lax.all_gather(line, axis), 0, [])  16.7 us
    ppermute x2, starting transfers between devices, with_halo(): lax.ppermute(initial, axis, [(b, a) for a, b in up])  13.2 us
    dot_general x4, matrix products, one_turn(): jnp.einsum('gn,knb->kgb', pick_source, stacked_all, preferred_element_typ...  10.2 us
    ppermute x2, starting transfers between devices, with_halo(): lax.ppermute(last, axis, up)  7.3 us
    reshape x1, local copies, waits for them, and re-layouts, near_field(): stacked_all = extended.reshape(extended.shape[0], 3 * leaves_here, leaf_len)  5.71 us
    dot_general x4, matrix products, one_turn(): jnp.einsum('gn,fnb->fgb', pick_target, center_points, preferred_element_t...  4.68 us
    concatenate x2, other arithmetic, with_halo(): jnp.concatenate([jnp.pad(low, around), array, jnp.pad(high, around)], axi...  3.34 us
  transfers between devices with their start and end apart: 5, of which 1 were waited for; matrix products, arithmetic and copies ran while one was open for 50% of the time, Pallas kernels for 0%

commit v1 on v0

v1 whole, which is shorter than its diff:
```python
import functools

import jax
import jax.numpy as jnp
from jax import lax
from jax.experimental import pallas as pl
from jax.experimental.pallas import tpu as pltpu
from jax.sharding import PartitionSpec as P

MESH = pl.DeviceIdType.MESH
LOG2E = 1.4426950408889634
f32 = jnp.float32
bf16 = jnp.bfloat16
NEAR_FIRST = (1, -1, 2, -2, 3, -3, 4)


def dot(a, b):
    return jnp.dot(a, b, preferred_element_type=f32)


def dot_nt(a, b):
    return lax.dot_general(a, b, (((1,), (1,)), ((), ())), preferred_element_type=f32)


def exchange_kernel(
    n_row,
    n_col,
    points,
    vectors,
    basis,
    transfer,
    node_transfer,
    halo_points,
    halo_vectors,
    window_moments,
    nodes_all,
    top_all,
    vec,
    bas,
    ltr,
    ntr,
    lifts,
    load_sem,
    near_node_send,
    near_node_recv,
    far_node_send,
    far_node_recv,
    lift_send,
    lift_recv,
    top_send,
    top_recv,
    pair_send,
    pair_recv,
    halo_send,
    halo_recv,
):
    n_z = n_col // 2
    row, col = lax.axis_index("row"), lax.axis_index("col")
    z, core = col // 2, col % 2
    devices = n_row * n_col
    me = row * n_col + col
    leaves = basis.shape[0]
    leaf = basis.shape[1]
    half = (leaves // 2) * leaf
    total = leaves * leaf

    def at(index):
        return {"row": index // n_col, "col": index % n_col}

    left = at((me + devices - 1) % devices)
    right = at((me + 1) % devices)
    partner = {"col": col + 1 - 2 * core}
    z_steps = [o % n_z for o in NEAR_FIRST if abs(o) <= n_z // 2]
    y_steps = [q % n_row for q in NEAR_FIRST if abs(q) <= n_row // 2]

    def z_peer(o):
        return {"col": ((z + o) % n_z) * 2 + core}

    def y_peer(q):
        return {"row": (row + q) % n_row}

    loads = [
        pltpu.make_async_copy(vectors, vec, load_sem.at[0]),
        pltpu.make_async_copy(basis, bas, load_sem.at[1]),
        pltpu.make_async_copy(transfer, ltr, load_sem.at[2]),
        pltpu.make_async_copy(node_transfer, ntr, load_sem.at[3]),
    ]
    for load in loads:
        load.start()
    barrier = pltpu.get_barrier_semaphore()
    peers = [left, right] + [z_peer(o) for o in z_steps] + [y_peer(q) for q in y_steps]
    for peer in peers:
        pl.semaphore_signal(barrier, inc=1, device_id=peer, device_id_type=MESH)

    def remote(src, dst, send, recv, device):
        return pltpu.make_async_remote_copy(
            src_ref=src,
            dst_ref=dst,
            send_sem=send,
            recv_sem=recv,
            device_id=device,
            device_id_type=MESH,
        )

    loads[0].wait()
    loads[1].wait()
    loads[2].wait()
    loads[3].wait()
    gathered = None
    for l in range(leaves):
        moment = dot(vec[:, l * leaf : (l + 1) * leaf], bas[l]).astype(bf16)
        window_moments[1, l] = moment
        part = dot(moment, ltr[l])
        gathered = part if gathered is None else gathered + part
    node = gathered.astype(bf16)
    nodes_all[core, row, z] = node
    lifts[row] = dot(node, ntr[0]).astype(bf16)
    pl.semaphore_wait(barrier, len(peers))

    started = []

    def go(copy):
        copy.start()
        started.append(copy)
        return copy

    def node_slot(o):
        return nodes_all.at[core, row, (z + n_z - o) % n_z]

    near_nodes = {}
    for o in z_steps:
        near_nodes[o] = go(
            remote(node_slot(0), node_slot(0), near_node_send.at[o], near_node_recv.at[o], z_peer(o))
        )
    far_nodes = {}

    def forward(o):
        for q in y_steps:
            far_nodes[o, q] = go(
                remote(
                    node_slot(o),
                    node_slot(o),
                    far_node_send.at[o, q],
                    far_node_recv.at[o, q],
                    y_peer(q),
                )
            )

    lifted = {}
    for q in y_steps:
        lifted[q] = go(
            remote(lifts.at[row], lifts.at[row], lift_send.at[q], lift_recv.at[q], y_peer(q))
        )
    forward(0)
    halos = []

    def send_halo(slot, src, to_left, to_right):
        halos.append(
            go(remote(src, to_left, halo_send.at[slot], halo_recv.at[slot], left))
        )
        halos.append(
            go(remote(src, to_right, halo_send.at[slot + 1], halo_recv.at[slot + 1], right))
        )

    send_halo(0, window_moments.at[1], window_moments.at[2], window_moments.at[0])
    first, second = pl.ds(0, half), pl.ds(half, total - half)
    send_halo(
        2, points.at[:, first], halo_points.at[1, :, first], halo_points.at[0, :, first]
    )
    for o in z_steps:
        near_nodes[o].wait_recv()
        forward(o)
    for q in y_steps:
        lifted[q].wait_recv()
    summed = lifts[0].astype(f32)
    for r in range(1, n_row):
        summed = summed + lifts[r].astype(f32)
    top_all[core, z] = summed.astype(bf16)
    tops = [
        go(remote(top_all.at[core, z], top_all.at[core, z], top_send.at[o], top_recv.at[o], z_peer(o)))
        for o in z_steps
    ]
    send_halo(
        4, points.at[:, second], halo_points.at[1, :, second], halo_points.at[0, :, second]
    )
    send_halo(6, vectors, halo_vectors.at[1], halo_vectors.at[0])
    pairs = []

    def give(slot, ref):
        pairs.append(go(remote(ref, ref, pair_send.at[slot], pair_recv.at[slot], partner)))

    give(0, nodes_all.at[core, row])
    for q in y_steps:
        for o in [0] + z_steps:
            far_nodes[o, q].wait_recv()
        give(q, nodes_all.at[core, (row + n_row - q) % n_row])
    for top in tops:
        top.wait_recv()
    give(n_row, top_all.at[core])
    for copy in pairs:
        copy.wait_recv()
    for copy in halos:
        copy.wait_recv()
    for copy in started:
        copy.wait_send()


def exchange(n_row, n_col, points, vectors, basis, transfer, node_transfer):
    leaves, leaf, rank = basis.shape
    columns = vectors.shape[0]
    n_z = n_col // 2
    anywhere = pl.BlockSpec(memory_space=pl.ANY)
    vmem = pl.BlockSpec(memory_space=pltpu.VMEM)
    dma = pltpu.SemaphoreType.DMA
    return pl.pallas_call(
        functools.partial(exchange_kernel, n_row, n_col),
        out_shape=(
            jax.ShapeDtypeStruct((2,) + points.shape, bf16),
            jax.ShapeDtypeStruct((2,) + vectors.shape, bf16),
            jax.ShapeDtypeStruct((3, leaves, columns, rank), bf16),
            jax.ShapeDtypeStruct((2, n_row, n_z, columns, rank), bf16),
            jax.ShapeDtypeStruct((2, n_z, columns, rank), bf16),
        ),
        in_specs=[anywhere] * 5,
        out_specs=(anywhere, anywhere, vmem, vmem, vmem),
        scratch_shapes=[
            pltpu.VMEM(vectors.shape, bf16),
            pltpu.VMEM(basis.shape, bf16),
            pltpu.VMEM(transfer.shape, bf16),
            pltpu.VMEM(node_transfer.shape, bf16),
            pltpu.VMEM((n_row, columns, rank), bf16),
            dma((4,)),
            dma((n_z,)),
            dma((n_z,)),
            dma((n_z, n_row)),
            dma((n_z, n_row)),
            dma((n_row,)),
            dma((n_row,)),
            dma((n_z,)),
            dma((n_z,)),
            dma((n_row + 1,)),
            dma((n_row + 1,)),
            dma((8,)),
            dma((8,)),
        ],
        compiler_params=pltpu.CompilerParams(collective_id=0, has_side_effects=True),
        name="exchange",
    )(points, vectors, basis, transfer, node_transfer)


def split3(value):
    high = value.astype(bf16).astype(f32)
    rest = value - high
    middle = rest.astype(bf16).astype(f32)
    return high, middle, rest - middle


def with_squares(block, scale, squares_at, ones_at, sign):
    wide = block.astype(f32)
    squares = sign * jnp.sum(wide * wide, axis=0, keepdims=True)
    high, middle, low = split3(squares)
    rows = lax.broadcasted_iota(jnp.int32, (16, block.shape[1]), 0)
    tail = jnp.where((rows >= ones_at) & (rows < ones_at + 3), sign, 0.0)
    tail = jnp.where(rows == squares_at, high, tail)
    tail = jnp.where(rows == squares_at + 1, middle, tail)
    tail = jnp.where(rows == squares_at + 2, low, tail)
    pad = jnp.zeros((128 - 16 - block.shape[0], block.shape[1]), bf16)
    return jnp.concatenate([(block * bf16(scale)), tail.astype(bf16), pad], axis=0)


def local_kernel(
    n_row,
    n_col,
    group,
    points,
    vectors,
    halo_points,
    halo_vectors,
    window_moments,
    nodes_all,
    top_all,
    basis,
    transfer,
    node_transfer,
    leaf_coupling,
    node_coupling,
    top_coupling,
    near_list,
    near_count,
    far_leaves,
    far_nodes,
    product,
    pts,
    vec,
    targets,
    near,
    mom,
    nod,
    top,
    bas,
    ltr,
    ntr,
    lcp,
    ncp,
    tcp,
    pair_target,
    pair_source,
    sem,
):
    leaves, leaf, rank = basis.shape
    features = points.shape[0]
    slots = near_list.shape[1]
    n_z = n_col // 2
    own = leaves * leaf
    me = lax.axis_index("row") * n_col + lax.axis_index("col")
    leaf_total = leaves * n_row * n_col
    window_start = (me - 1) * leaves

    def load(slot, src, dst):
        copy = pltpu.make_async_copy(src, dst, sem.at[slot])
        copy.start()
        return copy

    near_loads = [
        load(0, points, pts.at[:, pl.ds(own, own)]),
        load(1, halo_points.at[0], pts.at[:, pl.ds(0, own)]),
        load(2, halo_points.at[1], pts.at[:, pl.ds(2 * own, own)]),
        load(3, vectors, vec.at[:, pl.ds(own, own)]),
        load(4, halo_vectors.at[0], vec.at[:, pl.ds(0, own)]),
        load(5, halo_vectors.at[1], vec.at[:, pl.ds(2 * own, own)]),
    ]
    far_loads = [
        load(6, window_moments, mom),
        load(7, nodes_all, nod),
        load(8, top_all, top),
        load(9, leaf_coupling, lcp),
        load(10, node_coupling, ncp),
        load(11, top_coupling, tcp),
        load(12, node_transfer, ntr),
        load(13, transfer, ltr),
        load(14, basis, bas),
    ]

    def list_leaf(l, at):
        count = near_count[l]

        def list_slot(s, at):
            source = near_list[l, s] - window_start
            source = lax.select(source < 0, source + leaf_total, source)
            source = lax.select(source >= leaf_total, source - leaf_total, source)
            pair_target[at] = l
            pair_source[at] = source
            return at + 1

        return lax.fori_loop(0, count, list_slot, at)

    pairs = lax.fori_loop(0, leaves, list_leaf, 0)
    for extra in range(group - 1):
        pair_target[pairs + extra] = 0
        pair_source[pairs + extra] = leaves

    near[...] = jnp.zeros_like(near)
    near_loads[0].wait()

    def build(l, carry):
        at = pl.ds(pl.multiple_of(own + l * leaf, leaf), leaf)
        block = with_squares(pts[:, at], 2.0, 0, 3, -1.0)
        targets[l] = block.T
        return carry

    lax.fori_loop(0, leaves, build, 0)
    for copy in near_loads[1:]:
        copy.wait()

    tile = 256
    factor = LOG2E / (features / 2.0)

    def turn(g, carry):
        for member in range(group):
            index = g * group + member
            target = pair_target[index]
            source = pair_source[index]
            at = pl.ds(pl.multiple_of(source * leaf, leaf), leaf)
            weights = with_squares(pts[:, at], 1.0, 3, 0, 1.0)
            values = vec[:, at] * jnp.where(index < pairs, 1.0, 0.0).astype(bf16)
            for part in range(leaf // tile):
                lhs = targets[target, part * tile : (part + 1) * tile]
                kernel_tile = jnp.exp2(dot(lhs, weights) * factor).astype(bf16)
                near[target, :, part * tile : (part + 1) * tile] += dot_nt(values, kernel_tile)
        return carry

    lax.fori_loop(0, (pairs + group - 1) // group, turn, 0)

    for copy in far_loads:
        copy.wait()
    node_field = None
    for k in range(far_nodes.shape[1]):
        m = far_nodes[0, k]
        picked = nod[m % 2, m // n_col, (m % n_col) // 2]
        part = dot(picked, ncp[0, k])
        node_field = part if node_field is None else node_field + part
    top_field = None
    for j in range(n_col):
        part = dot(top[j % 2, j // 2], tcp[0, j])
        top_field = part if top_field is None else top_field + part
    node_down = (node_field + dot_nt(top_field.astype(bf16), ntr[0])).astype(bf16)
    for l in range(leaves):
        down = dot_nt(node_down, ltr[l])
        for k in range(far_leaves.shape[1]):
            j = far_leaves[l, k] - window_start
            j = lax.select(j < 0, j + leaf_total, j)
            j = lax.select(j >= leaf_total, j - leaf_total, j)
            down = down + dot(mom[j // leaves, j % leaves], lcp[l, k])
        far = dot_nt(down.astype(bf16), bas[l])
        product[:, l * leaf : (l + 1) * leaf] = (near[l] + far).astype(bf16)


def local_part(n_row, n_col, *arrays):
    (points, vectors, halo_points, halo_vectors, mom, nodes, top, basis, transfer) = arrays[:9]
    (node_transfer, leaf_coupling, node_coupling, top_coupling) = arrays[9:13]
    near_list = arrays[13]
    leaves, leaf, rank = basis.shape
    columns = vectors.shape[0]
    group = 2
    anywhere = pl.BlockSpec(memory_space=pl.ANY)
    smem = pl.BlockSpec(memory_space=pltpu.SMEM)
    vmem = pl.BlockSpec(memory_space=pltpu.VMEM)
    pairs = near_list.shape[0] * near_list.shape[1] + group
    return pl.pallas_call(
        functools.partial(local_kernel, n_row, n_col, group),
        out_shape=jax.ShapeDtypeStruct(vectors.shape, bf16),
        in_specs=[anywhere] * 13 + [smem] * 4,
        out_specs=vmem,
        scratch_shapes=[
            pltpu.VMEM((points.shape[0], 3 * points.shape[1]), bf16),
            pltpu.VMEM((columns, 3 * points.shape[1]), bf16),
            pltpu.VMEM((leaves, leaf, 128), bf16),
            pltpu.VMEM((leaves, columns, leaf), f32),
            pltpu.VMEM(mom.shape, bf16),
            pltpu.VMEM(nodes.shape, bf16),
            pltpu.VMEM(top.shape, bf16),
            pltpu.VMEM(basis.shape, bf16),
            pltpu.VMEM(transfer.shape, bf16),
            pltpu.VMEM(node_transfer.shape, bf16),
            pltpu.VMEM(leaf_coupling.shape, bf16),
            pltpu.VMEM(node_coupling.shape, bf16),
            pltpu.VMEM(top_coupling.shape, bf16),
            pltpu.SMEM((pairs,), jnp.int32),
            pltpu.SMEM((pairs,), jnp.int32),
            pltpu.SemaphoreType.DMA((15,)),
        ],
        name="local_part",
    )(*arrays)


def solution(mesh):
    n_row, n_col = mesh.shape["row"], mesh.shape["col"]

    def local(
        points,
        vectors,
        leaf_basis,
        leaf_transfer,
        node_transfer,
        leaf_coupling,
        node_coupling,
        top_coupling,
        near_list,
        near_count,
        far_leaves,
        far_nodes,
    ):
        halo_points, halo_vectors, moments, nodes, top = exchange(
            n_row, n_col, points, vectors, leaf_basis, leaf_transfer, node_transfer
        )
        return local_part(
            n_row,
            n_col,
            points,
            vectors,
            halo_points,
            halo_vectors,
            moments,
            nodes,
            top,
            leaf_basis,
            leaf_transfer,
            node_transfer,
            leaf_coupling,
            node_coupling,
            top_coupling,
            near_list,
            near_count,
            far_leaves,
            far_nodes,
        )

    return jax.shard_map(
        local,
        mesh=mesh,
        in_specs=(
            P(None, ("row", "col")),
            P("rhs", ("row", "col")),
            P(("row", "col"), None, None),
            P(("row", "col"), None, None),
            P(("row", "col"), None, None),
            P(("row", "col"), None, None, None),
            P(("row", "col"), None, None, None),
            P("col", None, None, None),
            P(("row", "col"), None),
            P(("row", "col")),
            P(("row", "col"), None),
            P(("row", "col"), None),
        ),
        out_specs=P("rhs", ("row", "col")),
        check_vma=False,
    )
```

time: 124 us -> 57.7 us (0.47)
  the two profiles are of different devices: /device:TPU:1 before, /device:TPU:6 now
where the time goes in v1:
time: 57.7 us; the launch traced here: 56.7 us
  Pallas kernels  54 us (94%)
  local copies, waits for them, and re-layouts  2.73 us (5%)
    pallas_call x1, Pallas kernels, exchange(): pl.pallas_call(functools.partial(exchange_kernel, n_row, n_col), out_shap...  36.6 us
    pallas_call x1, Pallas kernels, local_part(): pl.pallas_call(functools.partial(local_kernel, n_row, n_col, group), out_...  17.4 us
    unnamed x2, local copies, waits for them, and re-layouts  2.73 us

profile of v1, /device:TPU:6, one launch (start us, length us, event | category | flops | bytes accessed | tf_op | source)
XLA Modules:
  0.0 56.7 jit_solution(13292048084674750641)
XLA Ops:
  0.0 1.4 %copy.13.near_list = s32[12,5]{1,0:T(8,128)} copy(s32[12,5]{0,1:T(8,128)} %param.20) | data formatting | bytes 480 | tf_op args[8]
  1.4 1.4 %copy.14.far_leaves = s32[12,3]{1,0:T(8,128)} copy(s32[12,3]{0,1:T(4,128)} %param.22) | data formatting | bytes 288 | tf_op args[10]
  2.7 36.6 %exchange.1 = (bf16[2,64,6144]{2,1,0:T(8,128)(2,1)}, bf16[2,16,6144]{2,1,0:T(8,128)(2,1)}, bf16[3,12,16,128]{3,2,1,0:T(8,128)(2,1)}, bf16[2,8,8,16,128]{4,3,2,1,0:T(8,128)(2,1)}, bf16[2,8,16,128]{3,2,1,0:T(8,128)(2,1)}) custom-call(bf16[64,6144]{1,0:T(8,128)(2,1)} %points.3, bf16[16,6144]{1,0:T(8,128)(2,1)} %vectors.3, bf16[12,512,128]{2,1,0:T(8,128)(2,1)} %basis.3, ...), custom_call_target="tpu_custom_call" | custom-call | tf_op jit(solution)/shard_map/exchange/pallas_call | solution.py:215
  39.3 17.4 %local_part.1 = bf16[16,6144]{1,0:T(8,128)(2,1)} custom-call(bf16[64,6144]{1,0:T(8,128)(2,1)} %points.3, bf16[16,6144]{1,0:T(8,128)(2,1)} %vectors.3, bf16[2,64,6144]{2,1,0:T(8,128)(2,1)} %get-tuple-element.10.halo_points, bf16[2,16,6144]{2,1,0:T(8,128)(2,1)} %get-tuple-element.11.halo_vectors, bf16[3,12,16,128]{3,2,1,0:T(8,128)(2,1)} %get-tuple-element.12.window_moments, ...), custom_call_target="tpu_custom_call" | custom-call | tf_op jit(solution)/shard_map/local_part/pallas_call | solution.py:429
